TPU v7x, 32 devices: a whole 2x2x4 slice. The times are simulated.
32 devices in a mesh: row: 8 (over y, x, core), depth: 4 (over z).
Axes of the slice: x: 2, y: 2, z: 4, core: 2. Of those that a mesh axis runs over, the one named last changes fastest.
Arguments:
- l_cores: float32 [16, 32, 384, 384], P('row', 'depth'), may hold values from -0.0546875 to 0.0546875
- l_bucket: int32 [16, 32], P('row', 'depth'), may hold values from 1 to 3
- present: int32 [16, 32], P('row', 'depth'), may hold values 0 or 1
- u_cores: float32 [32, 4, 384, 384], P('depth', None, 'row'), may hold values from -6 to 6
- u_bucket: int32 [32, 4], P('depth'), may hold values from 1 to 3
- diag_cores: float32 [16, 4, 384, 384], P('row', None, 'depth'), may hold values from -6 to 6
- pivot_inv: float32 [4, 384, 384], P(None, 'row'), may hold values from -0.3125 to 0.3125
- coupling: float32 [3, 384, 384], P(None, 'row'), may hold values from -0.21875 to 0.21875
Outputs:
- finished: float32 [16, 4, 384, 384], P('row', None, 'depth')
Inputs may be any that keep to these rules, and one draw needn't show every extreme that they name: A lower tile's core rank is l_bucket * 128. An upper tile's core rank is u_bucket * 128. `present`: 1 marks a nonzero lower tile.
All inputs are finite; a program needn't handle non-finite values. No bound on the sum of `present` on one device may be relied on, other than what follows from the above.
Results may differ from a plain program's by a relative error of at most 0.0003.
Values sent between devices are 32-bit elements; how exact they have to be, the bound alone decides.
No kernel may reach another device: no remote copies, remote signals or barrier semaphores. Data moves between devices by JAX's collectives and lax.ppermute only.
A program may use at most 128 MiB of HBM per device.

v0:
```python
import jax
import jax.numpy as jnp
from jax import lax
from jax.sharding import PartitionSpec as P

HIGH = lax.Precision.HIGHEST


def per_device(l_cores, l_bucket, present, u_cores, u_bucket, diag_cores, pivot_inv, coupling):
    width = l_cores.shape[-1]
    rank_step = width // 3
    share_rows = diag_cores.shape[2]
    pivots, links = (
        lax.all_gather(pivot_inv, "row", axis=1, tiled=True),
        lax.all_gather(coupling, "row", axis=1, tiled=True),
    )
    positions = jnp.arange(width, dtype=jnp.int32)
    col_keep = (
        (positions[None, None, :] < (l_bucket * rank_step)[:, :, None]) & (present[:, :, None] > 0)
    ).astype(jnp.float32)
    l_masked = l_cores * col_keep[:, :, None, :]
    u_limits = u_bucket * rank_step
    portion = lax.all_gather(u_cores, "row", axis=2, tiled=True)
    count_rows = portion.shape[2]
    row_ids = jnp.arange(count_rows, dtype=jnp.int32)
    row_mask = (row_ids[None, None, :] < u_limits[:, :, None]).astype(jnp.float32)
    u_masked = portion * row_mask[..., None]
    partial_update = jnp.einsum("ikar,kjrb->ijab", l_masked, u_masked, precision=HIGH)
    summed = lax.psum(partial_update, "depth")
    own_rows = lax.dynamic_slice_in_dim(summed, lax.axis_index("depth") * share_rows, share_rows, 2)
    reduced = diag_cores - own_rows
    previous = jnp.einsum("iab,bc->iac", reduced[:, 0], pivots[0], precision=HIGH)
    results = [previous]
    for column in range(1, reduced.shape[1]):
        linked = jnp.einsum("iab,bc->iac", previous, links[column - 1], precision=HIGH)
        previous = jnp.einsum(
            "iab,bc->iac", reduced[:, column] - linked, pivots[column], precision=HIGH
        )
        results.append(previous)
    return jnp.stack(results, axis=1)


def solution(mesh):
    in_specs = (
        P("row", "depth", None, None),
        P("row", "depth"),
        P("row", "depth"),
        P("depth", None, "row", None),
        P("depth", None),
        P("row", None, "depth", None),
        P(None, "row", None),
        P(None, "row", None),
    )
    out_specs = P("row", None, "depth", None)
    return jax.shard_map(
        per_device, mesh=mesh, in_specs=in_specs, out_specs=out_specs, check_vma=False
    )
```

profile of v0, /device:TPU:0, one launch (start us, length us, event | category | flops | bytes accessed | tf_op | source)
XLA Modules:
  0.0 453.8 jit_solution(7917406552698786464)
XLA Ops:
  6.5 0.0 copy-start.2
  6.5 0.0 copy-start.4
  6.5 0.0 copy-start.3
  6.5 0.0 all-gather.4.cloned.1.call-start
  6.5 0.7 all-gather.4.cloned.1.call-update
  7.3 0.0 all-reduce.2.cloned.1.call-start
  7.3 0.0 copy-done.2
  7.3 0.1 copy.9
  7.4 0.0 copy-done.4
  7.4 0.0 copy-done.3
  7.4 0.1 fusion.15
  7.5 0.1 fusion.13
  7.6 103.0 %all-gather.4.cloned.1.call-done = f32[8,4,384,384]{3,2,1,0:T(8,128)} async-done(((f32[8,4,48,384]{3,2,1,0:T(8,128)}), f32[8,4,384,384]{3,2,1,0:T(8,128)}) %all-gather.4.cloned.1.call-update) | async-done | bytes 18874384 | tf_op jit(solution)/shard_map/all_gather | solution.py:23
  110.6 94.9 %fusion.5 = f32[2,4,384,384]{2,3,0,1:T(8,128)} fusion(f32[2,8,384,384]{3,2,1,0:T(8,128)} %param.8, f32[2,8,384]{2,1,0:T(8,128)S(1)} %fusion.15, f32[8,4,384,384]{3,2,1,0:T(8,128)} %all-gather.4.cloned.1.call-done, f32[8,4,384]{2,1,0:T(4,128)S(1)} %fusion.13), kind=kOutput, calls=%fused_computation.6 | convolution fusion | flops 43493621760 | bytes 33103872 | tf_op jit(solution)/shard_map/ikar,kjrb->ijab/dot_general | solution.py:28
  205.5 0.0 copy-start.1
  205.5 0.0 all-reduce.2.cloned.1.call-update
  205.5 0.0 all-gather.6.cloned.1.call-start
  205.6 0.7 all-gather.6.cloned.1.call-update
  206.3 0.0 all-gather.8.cloned.1.call-start
  206.3 0.5 all-gather.8.cloned.1.call-update
  206.9 0.0 copy-done.1
  206.9 0.5 copy.11
  207.3 170.3 %all-reduce.2.cloned.1.call-done = f32[2,4,384,384]{2,3,0,1:T(8,128)} async-done(((f32[2,4,384,384]{2,3,0,1:T(8,128)}), f32[2,4,384,384]{2,3,0,1:T(8,128)}) %all-reduce.2.cloned.1.call-update) | async-done | bytes 4718608 | tf_op jit(solution)/shard_map/psum | solution.py:29
  377.6 2.4 dynamic-slice_subtract_fusion
  380.0 27.4 %all-gather.6.cloned.1.call-done = f32[4,384,384]{2,1,0:T(8,128)} async-done(((f32[4,48,384]{2,1,0:T(8,128)}), f32[4,384,384]{2,1,0:T(8,128)}) %all-gather.6.cloned.1.call-update) | async-done | bytes 2359312 | tf_op jit(solution)/shard_map/all_gather | solution.py:14
  407.4 1.9 fusion.12
  409.4 26.3 %all-gather.8.cloned.1.call-done = f32[3,384,384]{2,1,0:T(8,128)} async-done(((f32[3,48,384]{2,1,0:T(8,128)}), f32[3,384,384]{2,1,0:T(8,128)}) %all-gather.8.cloned.1.call-update) | async-done | bytes 1769488 | tf_op jit(solution)/shard_map/all_gather | solution.py:15
  435.6 0.0 copy-start
  435.6 2.3 convolution_subtract_fusion.2
  437.9 2.0 fusion.11
  439.9 2.2 convolution_subtract_fusion.1
  442.1 0.0 copy-done
  442.1 0.9 fusion.10
  443.0 2.2 convolution_subtract_fusion
  445.2 0.9 convolution_bitcast_fusion
  446.1 0.1 pad_maximum_fusion
  446.2 1.1 copy.16
  (3 shorter events, 0.0 us)
Async XLA Ops:
  6.5 0.8 copy-start.2
  6.5 0.9 copy-start.4
  6.5 0.9 copy-start.3
  6.5 104.1 %all-gather.4.cloned.1.call-start = ((), (), s32[]{:S(2)}) async-start(), calls=%async_computation | async-start | bytes 21233664 | tf_op jit(solution)/shard_map/all_gather | solution.py:23
  7.3 370.4 %all-reduce.2.cloned.1.call-start = ((), (), s32[]{:S(2)}) async-start(), calls=%async_computation.1 | async-start | bytes 9437184 | tf_op jit(solution)/shard_map/psum | solution.py:29
  205.5 1.3 copy-start.1
  205.5 201.9 %all-gather.6.cloned.1.call-start = ((), (), s32[]{:S(2)}) async-start(), calls=%async_computation.2 | async-start | bytes 2654208 | tf_op jit(solution)/shard_map/all_gather | solution.py:14
  206.3 229.3 %all-gather.8.cloned.1.call-start = ((), (), s32[]{:S(2)}) async-start(), calls=%async_computation.3 | async-start | bytes 1990656 | tf_op jit(solution)/shard_map/all_gather | solution.py:15
  435.6 6.5 %copy-start = (f32[4,384,384]{2,1,0:T(8,128)S(1)}, f32[4,384,384]{2,1,0:T(8,128)}, u32[]{:S(2)}) copy-start(f32[4,384,384]{2,1,0:T(8,128)} %all-gather.6.cloned.1.call-done) | copy-start | bytes 7077892
Sparse Core Ops, SparseCore 0:
  9.2 101.3 all-gather.3
  205.7 171.9 all-reduce.1
  379.5 27.8 all-gather.5
  409.2 26.3 all-gather.7
where the time goes:
time: 454 us
  waiting for transfers between devices  329 us (72%)
  matrix products  107 us (24%)
  between operations  13.3 us (3%)
    psum x1, waiting for transfers between devices, per_device(): summed = lax.psum(partial_update, 'depth')  170 us
    all_gather x1, waiting for transfers between devices, per_device(): portion = lax.all_gather(u_cores, 'row', axis=2, tiled=True)  103 us
    dot_general x1, matrix products, per_device(): jnp.einsum('ikar,kjrb->ijab', l_masked, u_masked, precision=HIGH)  94.9 us
    all_gather x1, waiting for transfers between devices, per_device(): lax.all_gather(pivot_inv, 'row', axis=1, tiled=True)  27.4 us
    all_gather x1, waiting for transfers between devices, per_device(): lax.all_gather(coupling, 'row', axis=1, tiled=True)  26.3 us
  transfers between devices with their start and end apart: 4, of which 4 were waited for; matrix products, arithmetic and copies ran while one was open for 1% of the time, Pallas kernels for 0%

commit v1 on v0

--- a/solution.py
+++ b/solution.py
@@ -11,7 +11,7 @@
     rank_step = width // 3
     share_rows = diag_cores.shape[2]
     pivots, links = (
-        lax.all_gather(pivot_inv, "row", axis=1, tiled=True),
+        jnp.concatenate(lax.all_gather(pivot_inv, "row"), axis=1),
         lax.all_gather(coupling, "row", axis=1, tiled=True),
     )
     positions = jnp.arange(width, dtype=jnp.int32)

time: 454 us -> 420 us (0.925)
  waiting for transfers between devices: 329 us -> 295 us
    all_gather x1, waiting for transfers between devices: 27.4 us -> 0.02 us  [per_device(): lax.all_gather(pivot_inv, 'row')]
  transfers between devices with their start and end apart: 4 -> 4, of which waited for: 4 -> 3; matrix products, arithmetic and copies ran while one was open for 1% -> 24% of each run, Pallas kernels for 0% -> 0%
where the time goes in v1:
time: 420 us
  waiting for transfers between devices  295 us (70%)
  matrix products  103 us (25%)
  between operations  13.3 us (3%)
  local copies, waits for them, and re-layouts  5.66 us (1%)
    psum x1, waiting for transfers between devices, per_device(): summed = lax.psum(partial_update, 'depth')  167 us
    all_gather x1, waiting for transfers between devices, per_device(): portion = lax.all_gather(u_cores, 'row', axis=2, tiled=True)  102 us
    dot_general x1, matrix products, per_device(): jnp.einsum('ikar,kjrb->ijab', l_masked, u_masked, precision=HIGH)  94.9 us
    all_gather x1, waiting for transfers between devices, per_device(): lax.all_gather(coupling, 'row', axis=1, tiled=True)  23.8 us
  transfers between devices with their start and end apart: 4, of which 3 were waited for; matrix products, arithmetic and copies ran while one was open for 24% of the time, Pallas kernels for 0%

profile of v1, /device:TPU:0, one launch (start us, length us, event | category | flops | bytes accessed | tf_op | source)
XLA Modules:
  0.0 419.8 jit_solution(15169069880974969929)
XLA Ops:
  6.5 0.0 copy-start.6
  6.5 0.0 copy-start.8
  6.5 0.0 copy-start.7
  6.5 0.0 all-gather.5.cloned.1.call-start
  6.5 0.7 all-gather.5.cloned.1.call-update
  7.3 0.0 all-gather.9.cloned.1.call-start
  7.3 0.7 all-gather.9.cloned.1.call-update
  8.0 0.0 all-reduce.2.cloned.1.call-start
  8.1 0.0 copy-done.6
  8.1 0.1 copy.18
  8.2 0.0 copy-done.8
  8.2 0.0 copy-done.7
  8.2 0.1 fusion.13
  8.3 0.1 fusion.11
  8.3 102.3 %all-gather.5.cloned.1.call-done = f32[8,4,384,384]{3,2,1,0:T(8,128)} async-done(((f32[8,4,48,384]{3,2,1,0:T(8,128)}), f32[8,4,384,384]{3,2,1,0:T(8,128)}) %all-gather.5.cloned.1.call-update) | async-done | bytes 18874384 | tf_op jit(solution)/shard_map/all_gather | solution.py:23
  110.6 94.9 %fusion.5 = f32[2,4,384,384]{2,3,0,1:T(8,128)} fusion(f32[2,8,384,384]{3,2,1,0:T(8,128)} %param.8, f32[2,8,384]{2,1,0:T(8,128)S(1)} %fusion.13, f32[8,4,384,384]{3,2,1,0:T(8,128)} %all-gather.5.cloned.1.call-done, f32[8,4,384]{2,1,0:T(4,128)S(1)} %fusion.11), kind=kOutput, calls=%fused_computation.7 | convolution fusion | flops 43493621760 | bytes 33103872 | tf_op jit(solution)/shard_map/ikar,kjrb->ijab/dot_general | solution.py:28
  205.5 0.0 copy-start.5
  205.5 0.0 all-reduce.2.cloned.1.call-update
  205.5 0.0 all-gather.7.cloned.1.call-start
  205.6 0.5 all-gather.7.cloned.1.call-update
  206.1 0.7 copy-done.5
  206.8 0.5 copy.20
  207.2 0.0 all-gather.9.cloned.1.call-done
  207.3 1.8 copy.43
  209.1 1.5 fusion.14
  210.6 167.0 %all-reduce.2.cloned.1.call-done = f32[2,4,384,384]{2,3,0,1:T(8,128)} async-done(((f32[2,4,384,384]{2,3,0,1:T(8,128)}), f32[2,4,384,384]{2,3,0,1:T(8,128)}) %all-reduce.2.cloned.1.call-update) | async-done | bytes 4718608 | tf_op jit(solution)/shard_map/psum | solution.py:29
  377.6 0.0 copy-start.3
  377.6 2.4 dynamic-slice_subtract_fusion
  380.1 0.0 copy-start.2
  380.1 0.0 copy-done.3
  380.1 0.9 fusion.10
  381.0 23.8 %all-gather.7.cloned.1.call-done = f32[3,384,384]{2,1,0:T(8,128)} async-done(((f32[3,48,384]{2,1,0:T(8,128)}), f32[3,384,384]{2,1,0:T(8,128)}) %all-gather.7.cloned.1.call-update) | async-done | bytes 1769488 | tf_op jit(solution)/shard_map/all_gather | solution.py:15
  404.8 0.0 copy-start.4
  404.8 2.3 convolution_subtract_fusion.2
  407.1 0.0 copy-start.1
  407.1 0.0 copy-done.2
  407.1 0.9 fusion.15
  408.0 0.0 copy-done.4
  408.0 1.1 convolution_subtract_fusion.1
  409.2 0.0 copy-start
  409.2 0.0 copy-done.1
  409.2 0.9 fusion.16
  410.1 1.1 convolution_subtract_fusion
  411.2 0.0 copy-done
  411.2 0.9 convolution_bitcast_fusion
  412.1 0.1 pad_maximum_fusion
  412.2 1.1 copy.26
  (3 shorter events, 0.0 us)
Async XLA Ops:
  6.5 1.5 copy-start.6
  6.5 1.6 copy-start.8
  6.5 1.6 copy-start.7
  6.5 104.1 %all-gather.5.cloned.1.call-start = ((), (), s32[]{:S(2)}) async-start(), calls=%async_computation | async-start | bytes 21233664 | tf_op jit(solution)/shard_map/all_gather | solution.py:23
  7.3 200.0 %all-gather.9.cloned.1.call-start = ((), (), s32[]{:S(2)}) async-start(), calls=%async_computation.3 | async-start | bytes 2654208 | tf_op jit(solution)/shard_map/all_gather | solution.py:14
  8.0 369.6 %all-reduce.2.cloned.1.call-start = ((), (), s32[]{:S(2)}) async-start(), calls=%async_computation.1 | async-start | bytes 9437184 | tf_op jit(solution)/shard_map/psum | solution.py:29
  205.5 1.3 copy-start.5
  205.5 199.3 %all-gather.7.cloned.1.call-start = ((), (), s32[]{:S(2)}) async-start(), calls=%async_computation.2 | async-start | bytes 1990656 | tf_op jit(solution)/shard_map/all_gather | solution.py:15
  377.6 2.4 copy-start.3
  380.1 27.0 %copy-start.2 = (f32[1,8,48,384]{3,2,1,0:T(8,128)S(1)}, f32[1,8,48,384]{3,2,1,0:T(8,128)}, u32[]{:S(2)}) copy-start(f32[1,8,48,384]{3,2,1,0:T(8,128)} %get-tuple-element.7) | copy-start | bytes 1769476
  404.8 3.3 copy-start.4
  407.1 2.1 copy-start.1
  409.2 2.1 copy-start
Sparse Core Ops, SparseCore 0:
  9.2 101.3 all-gather.4
  112.5 28.8 all-gather.8
  205.7 171.9 all-reduce.1
  379.4 25.3 all-gather.6

commit v2 on v0

--- a/solution.py
+++ b/solution.py
@@ -26,7 +26,9 @@
     row_mask = (row_ids[None, None, :] < u_limits[:, :, None]).astype(jnp.float32)
     u_masked = portion * row_mask[..., None]
     partial_update = jnp.einsum("ikar,kjrb->ijab", l_masked, u_masked, precision=HIGH)
-    summed = lax.psum(partial_update, "depth")
+    summed = partial_update
+    for hop in (1, 2):
+        summed = summed + lax.ppermute(summed, "depth", [(dev, dev ^ hop) for dev in range(4)])
     own_rows = lax.dynamic_slice_in_dim(summed, lax.axis_index("depth") * share_rows, share_rows, 2)
     reduced = diag_cores - own_rows
     previous = jnp.einsum("iab,bc->iac", reduced[:, 0], pivots[0], precision=HIGH)

time: 454 us -> 502 us (1.11)
  waiting for transfers between devices: 329 us -> 409 us
  matrix products: 107 us -> 64.9 us
  other arithmetic: 2.6 us -> 8.49 us
    ppermute x0 -> x2, waiting for transfers between devices: none -> 306 us  [per_device(): lax.ppermute(summed, 'depth', [(dev, dev ^ hop) for dev in range(4)])]
    psum x1 -> x0, waiting for transfers between devices: 170 us -> none  [per_device(): summed = lax.psum(partial_update, 'depth')]
    dot_general x1, matrix products: 94.9 us -> 54.1 us  [per_device(): jnp.einsum('ikar,kjrb->ijab', l_masked, u_masked, precision=HIGH)]
    all_gather x1, waiting for transfers between devices: 27.4 us -> 0.02 us  [per_device(): lax.all_gather(pivot_inv, 'row', axis=1, tiled=True)]
    all_gather x1, waiting for transfers between devices: 26.3 us -> 0.02 us  [per_device(): lax.all_gather(coupling, 'row', axis=1, tiled=True)]
    add x0 -> x1, other arithmetic: none -> 6.45 us  [per_device(): summed + lax.ppermute(summed, 'depth', [(dev, dev ^ hop) for dev in range...]
  transfers between devices with their start and end apart: 4 -> 5, of which waited for: 4 -> 3; matrix products, arithmetic and copies ran while one was open for 1% -> 2% of each run, Pallas kernels for 0% -> 0%
where the time goes in v2:
time: 502 us; the launch traced here: 501 us
  waiting for transfers between devices  409 us (81%)
  matrix products  64.9 us (13%)
  between operations  13.2 us (3%)
  other arithmetic  8.49 us (2%)
    ppermute x2, waiting for transfers between devices, per_device(): lax.ppermute(summed, 'depth', [(dev, dev ^ hop) for dev in range(4)])  306 us
    all_gather x1, waiting for transfers between devices, per_device(): portion = lax.all_gather(u_cores, 'row', axis=2, tiled=True)  103 us
    dot_general x1, matrix products, per_device(): jnp.einsum('ikar,kjrb->ijab', l_masked, u_masked, precision=HIGH)  54.1 us
  transfers between devices with their start and end apart: 5, of which 3 were waited for; matrix products, arithmetic and copies ran while one was open for 2% of the time, Pallas kernels for 0%

profile of v2, /device:TPU:0, one launch (start us, length us, event | category | flops | bytes accessed | tf_op | source)
XLA Modules:
  0.0 501.3 jit_solution(4868546805948807584)
XLA Ops:
  6.5 0.0 copy-start.2
  6.5 0.0 copy-start.4
  6.5 0.0 copy-start.3
  6.5 0.0 all-gather.4.cloned.1.call-start
  6.5 0.7 all-gather.4.cloned.1.call-update
  7.3 0.0 all-gather.6.cloned.1.call-start
  7.3 0.0 copy-done.2
  7.3 0.1 copy.9
  7.4 0.0 copy-done.4
  7.4 0.0 copy-done.3
  7.4 0.1 fusion.25
  7.5 0.1 fusion.23
  7.6 103.0 %all-gather.4.cloned.1.call-done = f32[8,4,384,384]{3,2,1,0:T(8,128)} async-done(((f32[8,4,48,384]{3,2,1,0:T(8,128)}), f32[8,4,384,384]{3,2,1,0:T(8,128)}) %all-gather.4.cloned.1.call-update) | async-done | bytes 18874384 | tf_op jit(solution)/shard_map/all_gather | solution.py:23
  110.6 54.1 %fusion.5 = f32[2,4,384,384]{3,2,0,1:T(8,128)} fusion(f32[2,8,384,384]{3,2,1,0:T(8,128)} %param.8, f32[2,8,384]{2,1,0:T(8,128)S(1)} %fusion.25, f32[8,4,384,384]{3,2,1,0:T(8,128)} %all-gather.4.cloned.1.call-done, f32[8,4,384]{2,1,0:T(4,128)S(1)} %fusion.23), kind=kOutput, calls=%fused_computation.6 | convolution fusion | flops 43493621760 | bytes 33103872 | tf_op jit(solution)/shard_map/ikar,kjrb->ijab/dot_general | solution.py:28
  164.7 1.5 collective-permute-start
  166.2 0.0 all-gather.6.cloned.1.call-update
  166.2 0.0 copy-start.1
  166.2 0.0 all-gather.8.cloned.1.call-start
  166.3 102.7 %collective-permute-done = f32[2,4,384,384]{3,2,0,1:T(8,128)} collective-permute-done((f32[2,4,384,384]{3,2,0,1:T(8,128)}, f32[2,4,384,384]{3,2,0,1:T(8,128)}, u32[]{:S(2)}, u32[]{:S(2)}) %collective-permute-start) | collective-permute-done | bytes 4718624 | tf_op jit(solution)/shard_map/ppermute | solution.py:31
  269.0 6.4 %add.9 = f32[2,4,384,384]{3,2,0,1:T(8,128)} add(f32[2,4,384,384]{3,2,0,1:T(8,128)} %fusion.5, f32[2,4,384,384]{3,2,0,1:T(8,128)} %collective-permute-done) | non-fusion elementwise | flops 1179648 | bytes 14155776 | tf_op jit(solution)/shard_map/add | solution.py:31
  275.5 2.4 collective-permute-start.1
  277.9 0.0 all-gather.8.cloned.1.call-update
  277.9 203.0 %collective-permute-done.1 = f32[2,4,384,384]{3,2,0,1:T(8,128)} collective-permute-done((f32[2,4,384,384]{3,2,0,1:T(8,128)}, f32[2,4,384,384]{3,2,0,1:T(8,128)}, u32[]{:S(2)}, u32[]{:S(2)}) %collective-permute-start.1) | collective-permute-done | bytes 4718624 | tf_op jit(solution)/shard_map/ppermute | solution.py:31
  480.9 0.0 copy-done.1
  480.9 1.8 fusion.10
  482.7 0.0 all-gather.6.cloned.1.call-done
  482.7 1.8 fusion.16
  484.5 0.0 all-gather.8.cloned.1.call-done
  484.6 0.0 copy-start
  484.6 2.0 fusion.15
  486.6 1.8 fusion.14
  488.4 1.8 fusion.13
  490.2 0.0 copy-done
  490.2 0.8 fusion.12
  491.0 1.8 fusion.11
  492.8 0.8 convolution_bitcast_fusion
  493.6 0.1 pad_maximum_fusion
  493.7 1.1 copy.12
  (3 shorter events, 0.0 us)
Async XLA Ops:
  6.5 0.8 copy-start.2
  6.5 0.9 copy-start.4
  6.5 0.9 copy-start.3
  6.5 104.1 %all-gather.4.cloned.1.call-start = ((), (), s32[]{:S(2)}) async-start(), calls=%async_computation | async-start | bytes 21233664 | tf_op jit(solution)/shard_map/all_gather | solution.py:23
  7.3 475.5 %all-gather.6.cloned.1.call-start = ((), (), s32[]{:S(2)}) async-start(), calls=%async_computation.1 | async-start | bytes 2654208 | tf_op jit(solution)/shard_map/all_gather | solution.py:14
  164.7 104.3 %collective-permute-start = (f32[2,4,384,384]{3,2,0,1:T(8,128)}, f32[2,4,384,384]{3,2,0,1:T(8,128)}, u32[]{:S(2)}, u32[]{:S(2)}) collective-permute-start(f32[2,4,384,384]{3,2,0,1:T(8,128)} %fusion.5), channel_id=1, source_target_pairs={{0,1},{1,0},{2,3},{3,2},{4,5},{5,4},{6,7},{7,6},{8,9},{9,8},{10,11... | collective-permute-start | bytes 14155784 | tf_op jit(solution)/shard_map/ppermute | solution.py:31
  166.2 314.7 %copy-start.1 = (f32[2,4,96,384]{3,2,1,0:T(8,128)S(1)}, f32[2,4,96,384]{3,2,1,0:T(8,128)}, u32[]{:S(2)}) copy-start(f32[2,4,96,384]{3,2,1,0:T(8,128)} %param.13) | copy-start | bytes 3538948
  166.2 318.3 %all-gather.8.cloned.1.call-start = ((), (), s32[]{:S(2)}) async-start(), calls=%async_computation.2 | async-start | bytes 1990656 | tf_op jit(solution)/shard_map/all_gather | solution.py:15
  275.5 205.4 %collective-permute-start.1 = (f32[2,4,384,384]{3,2,0,1:T(8,128)}, f32[2,4,384,384]{3,2,0,1:T(8,128)}, u32[]{:S(2)}, u32[]{:S(2)}) collective-permute-start(f32[2,4,384,384]{3,2,0,1:T(8,128)} %add.9), channel_id=1, source_target_pairs={{0,2},{1,3},{2,0},{3,1},{4,6},{5,7},{6,4},{7,5},{8,10},{9,11},{10,... | collective-permute-start | bytes 14155784 | tf_op jit(solution)/shard_map/ppermute | solution.py:31
  484.6 5.6 %copy-start = (f32[4,384,384]{2,1,0:T(8,128)S(1)}, f32[4,384,384]{2,1,0:T(8,128)}, u32[]{:S(2)}) copy-start(f32[4,384,384]{2,1,0:T(8,128)} %all-gather.6.cloned.1.call-done) | copy-start | bytes 7077892
Sparse Core Ops, SparseCore 0:
  9.2 101.3 all-gather.3
  166.4 27.9 all-gather.5
  278.0 24.5 all-gather.7
